TPU v7x, 32 devices: a whole 2x2x4 slice. The times are simulated.
32 devices in a mesh: seq: 4 (over z), head: 4 (over y, core), batch: 2 (over x).
Axes of the slice: x: 2, y: 2, z: 4, core: 2. Of those that a mesh axis runs over, the one named last changes fastest.
Arguments:
- tokens: bfloat16 [8192, 2048], P(('batch', 'seq')), parts along dimension 0, may hold values from -6 to 6
- neighbor_bank: bfloat16 [128, 256, 2048], P(('batch', 'seq')), parts along dimension 0, may hold values from -2100 to 2100
- slots: int32 [128], P(('batch', 'seq')), parts along dimension 0, may hold values from 0 to 15
- w_query: bfloat16 [2048, 2048], P('seq', 'head'), may hold values from -0.125 to 0.125
- w_key: bfloat16 [2048, 2048], P('seq', 'head'), may hold values from -0.125 to 0.125
- w_value: bfloat16 [2048, 2048], P('seq', 'head'), may hold values from -0.125 to 0.125
- w_out: bfloat16 [2048, 2048], P('head', 'seq'), may hold values from -0.125 to 0.125
Outputs:
- cross_out: bfloat16 [8192, 2048], P(('batch', 'seq'), 'head'), parts along dimension 0
There are 2 independent parts, one for each index of `batch`. A program takes and returns all parts, laid end to end along the dimension named above; an argument that names none is the same for every part. Nothing has to cross between parts.
Inputs may be any that keep to these rules, and one draw needn't show every extreme that they name: Entry c picks row c // 16 * 16 + slots[c] of neighbor_bank.
All inputs are finite; a program needn't handle non-finite values.
Results may differ from a plain program's by a relative error of at most 0.006.
The roundings to bfloat16 on the way count: a program that leaves them out, or rounds other values in their place, can miss the bound.
Values may be sent and summed in bfloat16 or wider, within the bound.
A program may use at most 128 MiB of HBM per device.

v0:
```python
import math
import jax
import jax.numpy as jnp
from jax import lax
from jax.sharding import PartitionSpec as P

HEAD_DIM = 128


def passed_along(block, axis, distance):
    devices = range(lax.axis_size(axis))
    route = [(i - distance, i) for i in devices if i - distance in devices]
    return lax.ppermute(block, axis, route)


def attend(query_blocks, key_blocks, value_blocks):
    scores = jnp.einsum(
        "cmhd,cnhd->chmn", query_blocks, key_blocks, preferred_element_type=jnp.float32
    ) / math.sqrt(HEAD_DIM)
    peak_score = jnp.max(scores, axis=-1, keepdims=True)
    exponent = jnp.exp(scores - peak_score)
    weights = (exponent / jnp.sum(exponent, axis=-1, keepdims=True)).astype(jnp.bfloat16)
    blended = jnp.einsum(
        "chmn,cnhd->cmhd", weights, value_blocks, preferred_element_type=jnp.float32
    ).astype(jnp.bfloat16)
    return blended.reshape(blended.shape[0] * blended.shape[1], blended.shape[2] * blended.shape[3])


def fold_rows(source, shard_rows):
    return jnp.dot(source, shard_rows, preferred_element_type=jnp.float32)


def local(tokens, neighbor_bank, slots, w_query, w_key, w_value, w_out):
    tok_rows, model_width = tokens.shape
    block_count = neighbor_bank.shape[0]
    neighbor_rows = neighbor_bank.shape[1]
    block_len = tok_rows // block_count
    local_width = w_query.shape[1]
    local_heads = local_width // HEAD_DIM
    hidden = tokens.astype(jnp.float32)
    normed = (hidden * lax.rsqrt(jnp.mean(hidden * hidden, axis=-1, keepdims=True) + 1e-06)).astype(
        jnp.bfloat16
    )
    retrieved = jnp.take(neighbor_bank, slots, axis=0)
    arrived = passed_along(retrieved[block_count - 1], "seq", 1)
    context = jnp.concatenate([arrived[None], retrieved[: block_count - 1]], axis=0)
    context_flat = context.reshape(block_count * neighbor_rows, model_width)
    query_sum = fold_rows(normed, lax.all_gather(w_query, "seq", axis=0, tiled=True))
    key_sum = fold_rows(context_flat, lax.all_gather(w_key, "seq", axis=0, tiled=True))
    value_sum = fold_rows(context_flat, lax.all_gather(w_value, "seq", axis=0, tiled=True))
    query_blocks = query_sum.astype(jnp.bfloat16).reshape(
        block_count, block_len, local_heads, HEAD_DIM
    )
    key_blocks = key_sum.astype(jnp.bfloat16).reshape(
        block_count, neighbor_rows, local_heads, HEAD_DIM
    )
    value_blocks = value_sum.astype(jnp.bfloat16).reshape(
        block_count, neighbor_rows, local_heads, HEAD_DIM
    )
    attended = attend(query_blocks, key_blocks, value_blocks)
    every_head = lax.all_gather(attended, "head", axis=1, tiled=True)
    wide_rows = lax.all_gather(w_out, "seq", axis=1, tiled=True)
    own_columns = lax.all_to_all(wide_rows, "head", split_axis=1, concat_axis=0, tiled=True)
    return jnp.dot(every_head, own_columns, preferred_element_type=jnp.float32).astype(jnp.bfloat16)


def solution(mesh):
    in_specs = (
        P(("batch", "seq"), None),
        P(("batch", "seq"), None, None),
        P(("batch", "seq")),
        P("seq", "head"),
        P("seq", "head"),
        P("seq", "head"),
        P("head", "seq"),
    )
    out_specs = P(("batch", "seq"), "head")
    return jax.shard_map(local, mesh=mesh, in_specs=in_specs, out_specs=out_specs, check_vma=False)
```

profile of v0, /device:TPU:0, one launch (start us, length us, event | category | flops | bytes accessed | tf_op | source)
XLA Modules:
  0.0 271.8 jit_solution(8878170851766473111)
XLA Ops:
  10.1 13.1 %gather_fusion = bf16[16,256,2048]{2,1,0:T(8,128)(2,1)} fusion(bf16[16,256,2048]{2,1,0:T(8,128)(2,1)} %param.8, s32[1024]{0:T(1024)S(1)} %pad_clamp_fusion), kind=kCustom, calls=%fused_computation | custom fusion | bytes 33554496 | tf_op jit(solution)/shard_map/jit(_take)/gather | solution.py:44
  23.2 8.6 %broadcast_select_fusion = bf16[16,256,2048]{2,1,0:T(8,128)(2,1)S(1)} fusion(bf16[16,256,2048]{2,1,0:T(8,128)(2,1)} %gather_fusion, pred[16]{0:T(512)(128)(4,1)S(1)} %compare_and_fusion), kind=kLoop, calls=%fused_computation.3 | loop fusion | flops 8388608 | bytes 33554448 | tf_op jit(solution)/shard_map/jit(_take)/select_n | solution.py:44
  31.8 5.7 %copy-done = bf16[16,256,2048]{2,1,0:T(8,128)(2,1)} copy-done((bf16[16,256,2048]{2,1,0:T(8,128)(2,1)}, bf16[16,256,2048]{2,1,0:T(8,128)(2,1)S(1)}, u32[]{:S(2)}) %copy-start) | copy-done | bytes 16777240
  37.6 5.0 %collective-permute-start = (bf16[256,2048]{1,0:T(8,128)(2,1)S(1)}, bf16[256,2048]{1,0:T(8,128)(2,1)S(1)}, u32[]{:S(2)}, u32[]{:S(2)}) collective-permute-start(bf16[256,2048]{1,0:T(8,128)(2,1)S(1)} %slice_bitcast_fusion), channel_id=1, source_target_pairs={{0,8},{8,16},{16,24},{1,9},{9,17},{17,25},{2,10},{10,18},{18,26},{... | collective-permute-start | bytes 3145736 | tf_op jit(solution)/shard_map/ppermute | solution.py:13
  43.7 2.2 copy-done.1
  46.8 31.2 %collective-permute-done = bf16[256,2048]{1,0:T(8,128)(2,1)S(1)} collective-permute-done((bf16[256,2048]{1,0:T(8,128)(2,1)S(1)}, bf16[256,2048]{1,0:T(8,128)(2,1)S(1)}, u32[]{:S(2)}, u32[]{:S(2)}) %collective-permute-start) | collective-permute-done | bytes 1048608 | tf_op jit(solution)/shard_map/ppermute | solution.py:13
  78.0 6.6 %pad_maximum_fusion = bf16[16,256,2048]{2,1,0:T(8,128)(2,1)} fusion(bf16[15,256,2048]{2,1,0:T(8,128)(2,1)S(1)} %slice-done, bf16[1,256,2048]{2,1,0:T(8,128)(2,1)S(1)} %bitcast.28), kind=kLoop, calls=%fused_computation.2 | loop fusion | flops 8388608 | bytes 33554432 | tf_op jit(solution)/shard_map/concatenate | solution.py:46
  84.6 14.4 %convolution_convert_fusion = bf16[4096,512]{1,0:T(8,128)(2,1)} fusion(bf16[4096,2048]{1,0:T(8,128)(2,1)} %bitcast.21, bf16[2048,512]{1,0:T(8,128)(2,1)} %all-gather.10.cloned.1.call-done), kind=kOutput, calls=%fused_computation.8 | convolution fusion | flops 8592031744 | bytes 23068672 | tf_op jit(solution)/shard_map/dot_general | solution.py:30
  99.0 13.5 %all-gather.8.cloned.1.call-done = bf16[2048,512]{1,0:T(8,128)(2,1)} async-done(((bf16[512,512]{1,0:T(8,128)(2,1)}), bf16[2048,512]{1,0:T(8,128)(2,1)}) %all-gather.8.cloned.1.call-update) | async-done | bytes 2097168 | tf_op jit(solution)/shard_map/all_gather | solution.py:48
  112.5 5.2 %fusion.18 = bf16[1024,512]{1,0:T(8,128)(2,1)S(1)} fusion(bf16[2048,512]{1,0:T(8,128)(2,1)} %all-gather.8.cloned.1.call-done, bf16[1024,2048]{1,0:T(8,128)(2,1)} %param.7, f32[1024]{0:T(1024)S(1)} %add_rsqrt_fusion), kind=kOutput, calls=%fused_computation.23 | convolution fusion | flops 2154299392 | bytes 7344128 | tf_op jit(solution)/shard_map/dot_general | solution.py:30
  117.8 7.0 %reshape.36 = bf16[16,256,4,128]{3,2,1,0:T(4,128)(2,1)} reshape(bf16[4096,512]{1,0:T(8,128)(2,1)} %convolution_convert_fusion) | data formatting | bytes 8388608 | tf_op jit(solution)/shard_map/reshape | solution.py:54
  125.1 34.8 %all-gather.6.cloned.1.call-done = bf16[2048,512]{1,0:T(8,128)(2,1)} async-done(((bf16[512,512]{1,0:T(8,128)(2,1)}), bf16[2048,512]{1,0:T(8,128)(2,1)}) %all-gather.6.cloned.1.call-update) | async-done | bytes 2097168 | tf_op jit(solution)/shard_map/all_gather | solution.py:50
  159.9 14.4 %convolution_convert_fusion.1 = bf16[4096,512]{1,0:T(8,128)(2,1)} fusion(bf16[4096,2048]{1,0:T(8,128)(2,1)} %bitcast.22, bf16[2048,512]{1,0:T(8,128)(2,1)} %all-gather.6.cloned.1.call-done), kind=kOutput, calls=%fused_computation.9 | convolution fusion | flops 8592031744 | bytes 23068672 | tf_op jit(solution)/shard_map/dot_general | solution.py:30
  174.3 7.0 %reshape.34 = bf16[16,256,4,128]{3,2,1,0:T(4,128)(2,1)} reshape(bf16[4096,512]{1,0:T(8,128)(2,1)} %convolution_convert_fusion.1) | data formatting | bytes 8388608 | tf_op jit(solution)/shard_map/reshape | solution.py:57
  181.2 3.8 %fusion.7 = f32[16,4,64,256]{3,2,1,0:T(8,128)S(1)} fusion(bf16[16,256,4,128]{3,2,1,0:T(4,128)(2,1)} %reshape.36, bf16[16,64,4,128]{3,2,1,0:T(4,128)(2,1)S(1)} %reshape.35), kind=kOutput, calls=%fused_computation.13 | convolution fusion | flops 268435456 | bytes 9437184 | tf_op jit(solution)/shard_map/cmhd,cnhd->chmn/dot_general | solution.py:17
  185.0 2.0 copy-done.2
  187.0 1.6 fusion.33
  188.6 12.0 %fusion.21 = bf16[16,64,4,128]{3,1,2,0:T(8,128)(2,1)S(1)} fusion(bf16[16,256,4,128]{3,2,1,0:T(4,128)(2,1)} %reshape.34, f32[16,4,64]{2,1,0:T(4,128)S(1)} %fusion.33, f32[16,4,64,256]{3,2,1,0:T(8,128)} %copy-done.2), kind=kOutput, calls=%fused_computation.25 | convolution fusion | flops 274206976 | bytes 9453568 | tf_op jit(solution)/shard_map/chmn,cnhd->cmhd/dot_general | solution.py:23
  201.5 1.2 copy.33
  202.7 3.1 %all-gather.14.cloned.1.call-done = bf16[512,2048]{0,1:T(8,128)(2,1)} async-done(((bf16[512,512]{0,1:T(8,128)(2,1)}), bf16[512,2048]{0,1:T(8,128)(2,1)}) %all-gather.14.cloned.1.call-update) | async-done | bytes 2097168 | tf_op jit(solution)/shard_map/all_gather | solution.py:62
  205.8 48.4 %all_to_all.19 = bf16[512,4,512]{0,2,1:T(8,128)(2,1)S(1)} all-to-all(bf16[512,4,512]{0,2,1:T(8,128)(2,1)} %bitcast.26), channel_id=1, replica_groups=mesh['seq'=4,'head'=4,'batch'=2] {'head'}, dimensions={1} | all-to-all | bytes 4194304 | tf_op jit(solution)/shard_map/all_to_all | solution.py:63
  254.2 2.4 copy.20
  256.6 2.6 all-gather.12.cloned.1.call-done
  259.1 6.2 %convolution_convert_fusion.2 = bf16[1024,512]{1,0:T(8,128)(2,1)} fusion(bf16[1024,2048]{1,0:T(8,128)(2,1)} %all-gather.12.cloned.1.call-done, bf16[2048,512]{1,0:T(8,128)(2,1)} %bitcast.27), kind=kOutput, calls=%fused_computation.24 | convolution fusion | flops 2148007936 | bytes 7340032 | tf_op jit(solution)/shard_map/dot_general | solution.py:64
  (27 shorter events, 6.8 us)
Async XLA Ops:
  6.5 78.0 %all-gather.10.cloned.1.call-start = ((), (), s32[]{:S(2)}) async-start(), calls=%async_computation.3 | async-start | bytes 2621440 | tf_op jit(solution)/shard_map/all_gather | solution.py:49
  7.3 105.3 %all-gather.8.cloned.1.call-start = ((), (), s32[]{:S(2)}) async-start(), calls=%async_computation.2 | async-start | bytes 2621440 | tf_op jit(solution)/shard_map/all_gather | solution.py:48
  8.0 151.9 %all-gather.6.cloned.1.call-start = ((), (), s32[]{:S(2)}) async-start(), calls=%async_computation.1 | async-start | bytes 2621440 | tf_op jit(solution)/shard_map/all_gather | solution.py:50
  8.7 197.1 %all-gather.14.cloned.1.call-start = ((), (), s32[]{:S(2)}) async-start(), calls=%async_computation.5 | async-start | bytes 2621440 | tf_op jit(solution)/shard_map/all_gather | solution.py:62
  23.2 19.4 %copy-start.3 = (bf16[512,512]{1,0:T(8,128)(2,1)S(1)}, bf16[512,512]{1,0:T(8,128)(2,1)}, u32[]{:S(2)}) copy-start(bf16[512,512]{1,0:T(8,128)(2,1)} %param.13) | copy-start | bytes 1572868
  31.8 5.7 %copy-start = (bf16[16,256,2048]{2,1,0:T(8,128)(2,1)}, bf16[16,256,2048]{2,1,0:T(8,128)(2,1)S(1)}, u32[]{:S(2)}) copy-start(bf16[16,256,2048]{2,1,0:T(8,128)(2,1)S(1)} %broadcast_select_fusion) | copy-start | bytes 50331652
  37.6 40.4 %collective-permute-start = (bf16[256,2048]{1,0:T(8,128)(2,1)S(1)}, bf16[256,2048]{1,0:T(8,128)(2,1)S(1)}, u32[]{:S(2)}, u32[]{:S(2)}) collective-permute-start(bf16[256,2048]{1,0:T(8,128)(2,1)S(1)} %slice_bitcast_fusion), channel_id=1, source_target_pairs={{0,8},{8,16},{16,24},{1,9},{9,17},{17,25},{2,10},{10,18},{18,26},{... | collective-permute-start | bytes 3145736 | tf_op jit(solution)/shard_map/ppermute | solution.py:13
  43.6 215.5 %all-gather.12.cloned.1.call-start = ((), (), s32[]{:S(2)}) async-start(), calls=%async_computation.4 | async-start | bytes 5242880 | tf_op jit(solution)/shard_map/all_gather | solution.py:61
  43.7 2.2 copy-start.1
  43.7 34.3 %slice-start = ((bf16[16,256,2048]{2,1,0:T(8,128)(2,1)}), bf16[15,256,2048]{2,1,0:T(8,128)(2,1)S(1)}, s32[]{:S(2)}) async-start(bf16[16,256,2048]{2,1,0:T(8,128)(2,1)} %copy-done), calls=%async_computation.6 | async-start | bytes 31457280 | tf_op jit(solution)/shard_map/slice | solution.py:46
  185.0 2.0 copy-start.2
Sparse Core Ops, SparseCore 0:
  8.9 56.2 all-gather.9
  66.7 45.7 all-gather.7
  114.1 45.7 all-gather.5
  161.3 44.4 all-gather.13
  207.2 51.8 all-gather.11
where the time goes:
time: 272 us
  waiting for transfers between devices  87.4 us (32%)
  matrix products  56 us (21%)
  blocking collectives  48.4 us (18%)
  local copies, waits for them, and re-layouts  42.7 us (16%)
  other arithmetic  19 us (7%)
  between operations  13.2 us (5%)
  starting transfers between devices  5.13 us (2%)
    all_to_all x1, blocking collectives, local(): lax.all_to_all(wide_rows, 'head', split_axis=1, concat_axis=0, tiled=True)  48.4 us
    all_gather x1, waiting for transfers between devices, local(): lax.all_gather(w_value, 'seq', axis=0, tiled=True)  34.8 us
    dot_general x3, matrix products, fold_rows(): return jnp.dot(source, shard_rows, preferred_element_type=jnp.float32)  34 us
    ppermute x1, waiting for transfers between devices, passed_along(): return lax.ppermute(block, axis, route)  31.2 us
    all_gather x1, waiting for transfers between devices, local(): lax.all_gather(w_query, 'seq', axis=0, tiled=True)  13.5 us
    gather x1, local copies, waits for them, and re-layouts, local(): retrieved = jnp.take(neighbor_bank, slots, axis=0)  13.1 us
    unnamed x10, local copies, waits for them, and re-layouts  12.1 us
    dot_general x1, matrix products, attend(): jnp.einsum('chmn,cnhd->cmhd', weights, value_blocks, preferred_element_ty...  12 us
  transfers between devices with their start and end apart: 6, of which 5 were waited for; matrix products, arithmetic and copies ran while one was open for 37% of the time, Pallas kernels for 0%

commit v1 on v0

--- a/solution.py
+++ b/solution.py
@@ -5,6 +5,19 @@
 from jax.sharding import PartitionSpec as P
 
 HEAD_DIM = 128
+
+
+def collect(x, axis, dim):
+    ways = lax.axis_size(axis)
+    up = [(d, (d + 1) % ways) for d in range(ways)]
+    down = [(d, (d - 1) % ways) for d in range(ways)]
+    earlier, later = ([x], [x])
+    for _ in range(ways // 2):
+        earlier.append(lax.ppermute(earlier[-1], axis, up))
+    for _ in range((ways - 1) // 2):
+        later.append(lax.ppermute(later[-1], axis, down))
+    line = jnp.concatenate([*earlier[::-1], *later[1:]], axis=dim)
+    return jnp.roll(line, (lax.axis_index(axis) - ways // 2) * x.shape[dim], axis=dim)
 
 
 def passed_along(block, axis, distance):
@@ -47,7 +60,7 @@
     context_flat = context.reshape(block_count * neighbor_rows, model_width)
     query_sum = fold_rows(normed, lax.all_gather(w_query, "seq", axis=0, tiled=True))
     key_sum = fold_rows(context_flat, lax.all_gather(w_key, "seq", axis=0, tiled=True))
-    value_sum = fold_rows(context_flat, lax.all_gather(w_value, "seq", axis=0, tiled=True))
+    value_sum = fold_rows(context_flat, collect(w_value, "seq", 0))
     query_blocks = query_sum.astype(jnp.bfloat16).reshape(
         block_count, block_len, local_heads, HEAD_DIM
     )

time: 272 us -> 253 us (0.930)
  waiting for transfers between devices: 87.4 us -> 48.9 us
  local copies, waits for them, and re-layouts: 42.7 us -> 61.2 us
  matrix products: 56 us -> 52 us
  blocking collectives: 48.4 us -> 44.6 us
  starting transfers between devices: 5.13 us -> 8.33 us
  other arithmetic: 19 us -> 22 us
    ppermute x0 -> x3, waiting for transfers between devices: none -> 41.6 us  [the longest x2 41.6 us: collect(): earlier.append(lax.ppermute(earlier[-1], axis, up))]
    all_gather x1 -> x0, waiting for transfers between devices: 34.8 us -> none  [local(): lax.all_gather(w_value, 'seq', axis=0, tiled=True)]
    ppermute x1, waiting for transfers between devices: 31.2 us -> 0.01 us  [passed_along(): return lax.ppermute(block, axis, route)]
    all_gather x1, waiting for transfers between devices: 13.5 us -> 0.01 us  [local(): lax.all_gather(w_query, 'seq', axis=0, tiled=True)]
    slice x2 -> x1, local copies, waits for them, and re-layouts: 0.01 us -> 13.5 us  [local(): retrieved[:block_count - 1]]
    ppermute x0 -> x3, starting transfers between devices: none -> 6.61 us  [the longest x2 4.51 us: collect(): earlier.append(lax.ppermute(earlier[-1], axis, up))]
    dot_general x3, matrix products: 34 us -> 30 us  [fold_rows(): return jnp.dot(source, shard_rows, preferred_element_type=jnp.float32)]
    all_to_all x1, blocking collectives: 48.4 us -> 44.6 us  [local(): lax.all_to_all(wide_rows, 'head', split_axis=1, concat_axis=0, tiled=True)]
  transfers between devices with their start and end apart: 6 -> 8, of which waited for: 5 -> 3; matrix products, arithmetic and copies ran while one was open for 37% -> 46% of each run, Pallas kernels for 0% -> 0%
where the time goes in v1:
time: 253 us; the launch traced here: 250 us
  local copies, waits for them, and re-layouts  61.2 us (24%)
  matrix products  52 us (21%)
  waiting for transfers between devices  48.9 us (19%)
  blocking collectives  44.6 us (18%)
  other arithmetic  22 us (9%)
  between operations  13.3 us (5%)
  starting transfers between devices  8.33 us (3%)
    all_to_all x1, blocking collectives, local(): lax.all_to_all(wide_rows, 'head', split_axis=1, concat_axis=0, tiled=True)  44.6 us
    ppermute x2, waiting for transfers between devices, collect(): earlier.append(lax.ppermute(earlier[-1], axis, up))  41.6 us
    dot_general x3, matrix products, fold_rows(): return jnp.dot(source, shard_rows, preferred_element_type=jnp.float32)  30 us
    unnamed x21, local copies, waits for them, and re-layouts  15.8 us
    slice x1, local copies, waits for them, and re-layouts, local(): retrieved[:block_count - 1]  13.5 us
    gather x1, local copies, waits for them, and re-layouts, local(): retrieved = jnp.take(neighbor_bank, slots, axis=0)  13.2 us
    dot_general x1, matrix products, attend(): jnp.einsum('chmn,cnhd->cmhd', weights, value_blocks, preferred_element_ty...  12 us
    select_n x2, other arithmetic, local(): retrieved = jnp.take(neighbor_bank, slots, axis=0)  9.29 us
  transfers between devices with their start and end apart: 8, of which 3 were waited for; matrix products, arithmetic and copies ran while one was open for 46% of the time, Pallas kernels for 0%

profile of v1, /device:TPU:0, one launch (start us, length us, event | category | flops | bytes accessed | tf_op | source)
XLA Modules:
  0.0 250.2 jit_solution(359847987553498771)
XLA Ops:
  7.3 3.1 %collective-permute-start.1 = (bf16[512,512]{1,0:T(8,128)(2,1)}, bf16[512,512]{1,0:T(8,128)(2,1)S(1)}, u32[]{:S(2)}, u32[]{:S(2)}) collective-permute-start(bf16[512,512]{1,0:T(8,128)(2,1)} %param.12), channel_id=1, source_target_pairs={{0,8},{8,16},{16,24},{24,0},{1,9},{9,17},{17,25},{25,1},{2,10},{10... | collective-permute-start | bytes 1572872 | tf_op jit(solution)/shard_map/ppermute | solution.py:16
  10.4 2.1 collective-permute-start.3
  13.2 13.2 %gather_fusion = bf16[16,256,2048]{2,1,0:T(8,128)(2,1)} fusion(bf16[16,256,2048]{2,1,0:T(8,128)(2,1)} %param.8, s32[1024]{0:T(1024)S(1)} %pad_clamp_fusion), kind=kCustom, calls=%fused_computation | custom fusion | bytes 33554496 | tf_op jit(solution)/shard_map/jit(_take)/gather | solution.py:57
  26.5 8.6 %broadcast_select_fusion = bf16[16,256,2048]{2,1,0:T(8,128)(2,1)S(1)} fusion(bf16[16,256,2048]{2,1,0:T(8,128)(2,1)} %gather_fusion, pred[16]{0:T(512)(128)(4,1)S(1)} %compare_and_fusion), kind=kLoop, calls=%fused_computation.3 | loop fusion | flops 8388608 | bytes 33554448 | tf_op jit(solution)/shard_map/jit(_take)/select_n | solution.py:57
  35.2 5.7 %copy-done = bf16[16,256,2048]{2,1,0:T(8,128)(2,1)} copy-done((bf16[16,256,2048]{2,1,0:T(8,128)(2,1)}, bf16[16,256,2048]{2,1,0:T(8,128)(2,1)S(1)}, u32[]{:S(2)}) %copy-start) | copy-done | bytes 16777240
  41.9 1.6 collective-permute-start
  44.6 13.5 %slice.11 = bf16[15,256,2048]{2,1,0:T(8,128)(2,1)} slice(bf16[16,256,2048]{2,1,0:T(8,128)(2,1)} %copy-done), slice={[0:15], [0:256], [0:2048]} | slice | bytes 31457280 | tf_op jit(solution)/shard_map/slice | solution.py:59
  59.5 3.1 %fusion.1 = f32[1024]{0:T(1024)S(1)} fusion(bf16[1024,2048]{1,0:T(8,128)(2,1)} %param.7), kind=kLoop, calls=%fused_computation.6 | loop fusion | flops 6290432 | bytes 4198400 | tf_op jit(solution)/shard_map/reduce_sum | solution.py:54
  62.6 41.6 %collective-permute-done.2 = bf16[512,512]{1,0:T(8,128)(2,1)S(1)} collective-permute-done((bf16[512,512]{1,0:T(8,128)(2,1)S(1)}, bf16[512,512]{1,0:T(8,128)(2,1)S(1)}, u32[]{:S(2)}, u32[]{:S(2)}) %collective-permute-start.2) | collective-permute-done | bytes 524320 | tf_op jit(solution)/shard_map/ppermute | solution.py:16
  104.5 8.0 %pad_maximum_fusion = bf16[16,256,2048]{2,1,0:T(8,128)(2,1)S(1)} fusion(bf16[15,256,2048]{2,1,0:T(8,128)(2,1)} %slice.11, bf16[1,256,2048]{2,1,0:T(8,128)(2,1)S(1)} %bitcast.27), kind=kLoop, calls=%fused_computation.2 | loop fusion | flops 8388608 | bytes 33554432 | tf_op jit(solution)/shard_map/concatenate | solution.py:59
  112.6 5.7 %copy-done.1 = bf16[16,256,2048]{2,1,0:T(8,128)(2,1)} copy-done((bf16[16,256,2048]{2,1,0:T(8,128)(2,1)}, bf16[16,256,2048]{2,1,0:T(8,128)(2,1)S(1)}, u32[]{:S(2)}) %copy-start.1) | copy-done | bytes 16777240
  118.3 10.4 %convolution_convert_fusion.1 = bf16[4096,512]{1,0:T(8,128)(2,1)} fusion(bf16[4096,2048]{1,0:T(8,128)(2,1)S(1)} %bitcast.20, bf16[4096,512]{1,0:T(8,128)(2,1)S(1)} %constant_dynamic-update-slice_fusion, s32[]{:T(128)S(6)} %select_n.25), kind=kOutput, calls=%fused_computation.9 | convolution fusion | flops 8592031744 | bytes 23068676 | tf_op jit(solution)/shard_map/dot_general | solution.py:43
  128.7 6.9 %reshape.34 = bf16[16,256,4,128]{3,2,1,0:T(4,128)(2,1)} reshape(bf16[4096,512]{1,0:T(8,128)(2,1)} %convolution_convert_fusion.1) | data formatting | bytes 8388608 | tf_op jit(solution)/shard_map/reshape | solution.py:70
  135.6 14.4 %convolution_convert_fusion = bf16[4096,512]{1,0:T(8,128)(2,1)} fusion(bf16[4096,2048]{1,0:T(8,128)(2,1)} %bitcast.21, bf16[2048,512]{1,0:T(8,128)(2,1)} %all-gather.7.cloned.1.call-done), kind=kOutput, calls=%fused_computation.8 | convolution fusion | flops 8592031744 | bytes 23068672 | tf_op jit(solution)/shard_map/dot_general | solution.py:43
  150.0 6.9 %reshape.36 = bf16[16,256,4,128]{3,2,1,0:T(4,128)(2,1)} reshape(bf16[4096,512]{1,0:T(8,128)(2,1)} %convolution_convert_fusion) | data formatting | bytes 8388608 | tf_op jit(solution)/shard_map/reshape | solution.py:67
  156.9 5.3 %fusion.19 = bf16[1024,512]{1,0:T(8,128)(2,1)S(1)} fusion(bf16[2048,512]{1,0:T(8,128)(2,1)} %all-gather.5.cloned.1.call-done, bf16[1024,2048]{1,0:T(8,128)(2,1)} %param.7, f32[1024]{0:T(1024)S(1)} %add_rsqrt_fusion), kind=kOutput, calls=%fused_computation.24 | convolution fusion | flops 2154299392 | bytes 7344128 | tf_op jit(solution)/shard_map/dot_general | solution.py:43
  162.7 3.8 %fusion.7 = f32[16,4,64,256]{3,2,1,0:T(8,128)S(1)} fusion(bf16[16,256,4,128]{3,2,1,0:T(4,128)(2,1)} %reshape.36, bf16[16,64,4,128]{3,2,1,0:T(4,128)(2,1)S(1)} %reshape.35), kind=kOutput, calls=%fused_computation.13 | convolution fusion | flops 268435456 | bytes 9437184 | tf_op jit(solution)/shard_map/cmhd,cnhd->chmn/dot_general | solution.py:30
  166.5 1.9 copy-done.2
  168.4 1.6 fusion.35
  170.0 12.0 %fusion.22 = bf16[16,64,4,128]{3,1,2,0:T(8,128)(2,1)S(1)} fusion(bf16[16,256,4,128]{3,2,1,0:T(4,128)(2,1)} %reshape.34, f32[16,4,64]{2,1,0:T(4,128)S(1)} %fusion.35, f32[16,4,64,256]{3,2,1,0:T(8,128)} %copy-done.2), kind=kOutput, calls=%fused_computation.26 | convolution fusion | flops 274206976 | bytes 9453568 | tf_op jit(solution)/shard_map/chmn,cnhd->cmhd/dot_general | solution.py:36
  184.2 44.6 %all_to_all.19 = bf16[512,4,512]{0,2,1:T(8,128)(2,1)S(1)} all-to-all(bf16[512,4,512]{0,2,1:T(8,128)(2,1)} %bitcast.25), channel_id=1, replica_groups=mesh['seq'=4,'head'=4,'batch'=2] {'head'}, dimensions={1} | all-to-all | bytes 4194304 | tf_op jit(solution)/shard_map/all_to_all | solution.py:76
  228.8 2.4 copy.20
  231.1 6.4 %all-gather.9.cloned.1.call-done = bf16[1024,2048]{1,0:T(8,128)(2,1)} async-done(((bf16[1024,512]{1,0:T(8,128)(2,1)}), bf16[1024,2048]{1,0:T(8,128)(2,1)}) %all-gather.9.cloned.1.call-update) | async-done | bytes 4194320 | tf_op jit(solution)/shard_map/all_gather | solution.py:74
  237.5 6.2 %convolution_convert_fusion.2 = bf16[1024,512]{1,0:T(8,128)(2,1)} fusion(bf16[1024,2048]{1,0:T(8,128)(2,1)} %all-gather.9.cloned.1.call-done, bf16[2048,512]{1,0:T(8,128)(2,1)} %bitcast.26), kind=kOutput, calls=%fused_computation.25 | convolution fusion | flops 2148007936 | bytes 7340032 | tf_op jit(solution)/shard_map/dot_general | solution.py:77
  (41 shorter events, 8.0 us)
Async XLA Ops:
  6.5 129.1 %all-gather.7.cloned.1.call-start = ((), (), s32[]{:S(2)}) async-start(), calls=%async_computation.2 | async-start | bytes 2621440 | tf_op jit(solution)/shard_map/all_gather | solution.py:62
  7.3 149.7 %all-gather.5.cloned.1.call-start = ((), (), s32[]{:S(2)}) async-start(), calls=%async_computation.1 | async-start | bytes 2621440 | tf_op jit(solution)/shard_map/all_gather | solution.py:61
  7.3 50.8 %collective-permute-start.1 = (bf16[512,512]{1,0:T(8,128)(2,1)}, bf16[512,512]{1,0:T(8,128)(2,1)S(1)}, u32[]{:S(2)}, u32[]{:S(2)}) collective-permute-start(bf16[512,512]{1,0:T(8,128)(2,1)} %param.12), channel_id=1, source_target_pairs={{0,8},{8,16},{16,24},{24,0},{1,9},{9,17},{17,25},{25,1},{2,10},{10... | collective-permute-start | bytes 1572872 | tf_op jit(solution)/shard_map/ppermute | solution.py:16
  10.4 93.9 %collective-permute-start.3 = (bf16[512,512]{1,0:T(8,128)(2,1)}, bf16[512,512]{1,0:T(8,128)(2,1)S(1)}, u32[]{:S(2)}, u32[]{:S(2)}) collective-permute-start(bf16[512,512]{1,0:T(8,128)(2,1)} %param.12), channel_id=1, source_target_pairs={{0,24},{8,0},{16,8},{24,16},{1,25},{9,1},{17,9},{25,17},{2,26},{10... | collective-permute-start | bytes 1572872 | tf_op jit(solution)/shard_map/ppermute | solution.py:18
  12.5 171.7 %all-gather.11.cloned.1.call-start = ((), (), s32[]{:S(2)}) async-start(), calls=%async_computation.4 | async-start | bytes 2621440 | tf_op jit(solution)/shard_map/all_gather | solution.py:75
  13.2 13.3 %copy-start.5 = (s32[16]{0:T(128)S(1)}, s32[16]{0:T(128)}, u32[]{:S(2)}) copy-start(s32[16]{0:T(128)} %param.9) | copy-start | bytes 196
  26.5 17.0 %copy-start.4 = (bf16[512,512]{1,0:T(8,128)(2,1)S(1)}, bf16[512,512]{1,0:T(8,128)(2,1)}, u32[]{:S(2)}) copy-start(bf16[512,512]{1,0:T(8,128)(2,1)} %param.13) | copy-start | bytes 1572868
  35.2 5.7 %copy-start = (bf16[16,256,2048]{2,1,0:T(8,128)(2,1)}, bf16[16,256,2048]{2,1,0:T(8,128)(2,1)S(1)}, u32[]{:S(2)}) copy-start(bf16[16,256,2048]{2,1,0:T(8,128)(2,1)S(1)} %broadcast_select_fusion) | copy-start | bytes 50331652
  41.9 62.6 %collective-permute-start = (bf16[256,2048]{1,0:T(8,128)(2,1)}, bf16[256,2048]{1,0:T(8,128)(2,1)S(1)}, u32[]{:S(2)}, u32[]{:S(2)}) collective-permute-start(bf16[256,2048]{1,0:T(8,128)(2,1)} %slice_bitcast_fusion), channel_id=1, source_target_pairs={{0,8},{8,16},{16,24},{1,9},{9,17},{17,25},{2,10},{10,18},{18,26},{... | collective-permute-start | bytes 3145736 | tf_op jit(solution)/shard_map/ppermute | solution.py:26
  44.6 192.9 %all-gather.9.cloned.1.call-start = ((), (), s32[]{:S(2)}) async-start(), calls=%async_computation.3 | async-start | bytes 5242880 | tf_op jit(solution)/shard_map/all_gather | solution.py:74
  58.1 46.2 %copy-start.3 = (bf16[512,512]{1,0:T(8,128)(2,1)S(1)}, bf16[512,512]{1,0:T(8,128)(2,1)}, u32[]{:S(2)}) copy-start(bf16[512,512]{1,0:T(8,128)(2,1)} %param.12) | copy-start | bytes 1572868
  58.1 46.1 %collective-permute-start.2 = (bf16[512,512]{1,0:T(8,128)(2,1)S(1)}, bf16[512,512]{1,0:T(8,128)(2,1)S(1)}, u32[]{:S(2)}, u32[]{:S(2)}) collective-permute-start(bf16[512,512]{1,0:T(8,128)(2,1)S(1)} %collective-permute-done.1), channel_id=1, source_target_pairs={{0,8},{8,16},{16,24},{24,0},{1,9},{9,17},{17,25},{25,1},{2,10},{10... | collective-permute-start | bytes 1572872 | tf_op jit(solution)/shard_map/ppermute | solution.py:16
  112.5 5.7 %copy-start.1 = (bf16[16,256,2048]{2,1,0:T(8,128)(2,1)}, bf16[16,256,2048]{2,1,0:T(8,128)(2,1)S(1)}, u32[]{:S(2)}) copy-start(bf16[16,256,2048]{2,1,0:T(8,128)(2,1)S(1)} %pad_maximum_fusion) | copy-start | bytes 50331652
  166.5 2.0 copy-start.2
Sparse Core Ops, SparseCore 0:
  8.9 78.4 all-gather.6
  89.0 46.2 all-gather.4
  136.8 47.3 all-gather.10
  185.6 51.8 all-gather.8
